TPU v7x, 16 devices: a whole 2x2x2 slice. The times are simulated.
16 devices in a mesh: tp: 2 (over z), dp: 8 (over y, x, core).
Axes of the slice: x: 2, y: 2, z: 2, core: 2. Of those that a mesh axis runs over, the one named last changes fastest.
Arguments:
- hid_q: bfloat16 [128, 512, 1024], P('dp')
- hid_d: bfloat16 [512, 512, 1024], P('dp')
- len_q: int32 [128], P('dp')
- len_d: int32 [512], P('dp')
- pos_doc: int32 [128], P('dp')
- w_q: bfloat16 [1024, 2048], P(None, 'tp')
- w_k: bfloat16 [1024, 1024], P(None, 'tp')
- w_v: bfloat16 [1024, 1024], P(None, 'tp')
- w_o: bfloat16 [2048, 1024], P('tp')
- w_gate: bfloat16 [1024, 3072], P(None, 'tp')
- w_up: bfloat16 [1024, 3072], P(None, 'tp')
- w_down: bfloat16 [3072, 1024], P('tp')
- g_in: bfloat16 [1024], replicated
- g_q: bfloat16 [128], replicated
- g_k: bfloat16 [128], replicated
- g_post: bfloat16 [1024], replicated
- g_final: bfloat16 [1024], replicated
Outputs:
- output 1: float32 [128], P('dp')
- output 2: bfloat16 [128, 512, 1024], P('dp')
- output 3: bfloat16 [512, 512, 1024], P('dp')
- output 4: float32 [1024, 2048], P(None, 'tp')
- output 5: float32 [1024, 1024], P(None, 'tp')
- output 6: float32 [1024, 1024], P(None, 'tp')
- output 7: float32 [2048, 1024], P('tp')
- output 8: float32 [1024, 3072], P(None, 'tp')
- output 9: float32 [1024, 3072], P(None, 'tp')
- output 10: float32 [3072, 1024], P('tp')
- output 11: float32 [1024], replicated
- output 12: float32 [128], replicated
- output 13: float32 [128], replicated
- output 14: float32 [1024], replicated
- output 15: float32 [1024], replicated
All inputs are finite; a program needn't handle non-finite values.
Results may differ from a plain program's by a relative error of at most 0.02.
Values sent between devices are 32-bit elements.
A program may use at most 1 GiB of HBM per device.

v0:
```python
import functools
import jax
import jax.numpy as jnp
from jax import lax
from jax.sharding import PartitionSpec as P

NORM_EPS = 1e-6
ROPE_THETA = 1000000.0
value_a11 = 0.05


def norm_rows(values, gain_vec):
    return values * lax.rsqrt(jnp.mean(values * values, axis=-1, keepdims=True) + NORM_EPS) * gain_vec


def norm_back(values, gain_vec, d_out):
    scale = lax.rsqrt(jnp.mean(values * values, axis=-1, keepdims=True) + NORM_EPS)
    g_dout = d_out * gain_vec
    d_values = scale * g_dout - values * scale ** 3 * jnp.mean(values * g_dout, axis=-1, keepdims=True)
    d_gain = jnp.sum((d_out * values * scale).reshape(-1, values.shape[-1]), axis=0)
    return d_values, d_gain


def rotate(values, angles):
    half_dim = values.shape[-1] // 2
    first_half = values[..., :half_dim]
    second_half = values[..., half_dim:]
    cos_a = jnp.cos(angles)
    sin_a = jnp.sin(angles)
    return jnp.concatenate([first_half * cos_a - second_half * sin_a, second_half * cos_a + first_half * sin_a], axis=-1)


def attend(q_raw, k_raw, v_raw, g_q, g_k, lens):
    head_dim = g_q.shape[0]
    n_seq, seq_len, kv_width = k_raw.shape
    n_kv = kv_width // head_dim
    group_size = q_raw.shape[1] // kv_width
    inv_freq = ROPE_THETA ** (-jnp.arange(0, head_dim, 2, dtype=jnp.float32) / head_dim)
    key_angle = jnp.arange(seq_len, dtype=jnp.float32)[:, None] * inv_freq
    key_rot = norm_rows(k_raw.reshape(n_seq, seq_len, n_kv, head_dim).astype(jnp.float32), g_k)
    key_rot = rotate(key_rot, key_angle[None, :, None, :]).astype(jnp.bfloat16)
    q_angle = (lens - 1).astype(jnp.float32)[:, None] * inv_freq
    query_rot = norm_rows(q_raw.reshape(n_seq, n_kv, group_size, head_dim).astype(jnp.float32), g_q)
    query_rot = rotate(query_rot, q_angle[:, None, None, :]).astype(jnp.bfloat16)
    scores = jnp.einsum('nkgd,nskd->nkgs', query_rot, key_rot, preferred_element_type=jnp.float32) * head_dim ** -0.5
    key_valid = jnp.arange(seq_len)[None, :] < lens[:, None]
    scores = jnp.where(key_valid[:, None, None, :], scores, -1e30)
    attn_prob = jax.nn.softmax(scores, axis=-1).astype(jnp.bfloat16)
    val_heads = v_raw.reshape(n_seq, seq_len, n_kv, head_dim)
    attn_mix = jnp.einsum('nkgs,nskd->nkgd', attn_prob, val_heads, preferred_element_type=jnp.float32)
    return attn_mix.astype(jnp.bfloat16).reshape(n_seq, q_raw.shape[1])


def swiglu(gate_in, up_in):
    return jax.nn.silu(gate_in) * up_in


def final_head(h_out, g_final):
    z_norm = norm_rows(h_out, g_final)
    return z_norm * lax.rsqrt(jnp.sum(z_norm * z_norm, axis=-1, keepdims=True))


def embed_fwd(hidden, lens, weights):
    w_q, w_k, w_v, w_o, w_gate, w_up, w_down, g_in, g_q, g_k, g_post, g_final = weights
    seq_len = hidden.shape[1]
    x_norm = norm_rows(hidden.astype(jnp.float32), g_in).astype(jnp.bfloat16)
    k_raw = jnp.einsum('nsd,de->nse', x_norm, w_k, preferred_element_type=jnp.float32).astype(jnp.bfloat16)
    v_raw = jnp.einsum('nsd,de->nse', x_norm, w_v, preferred_element_type=jnp.float32).astype(jnp.bfloat16)
    at_last = jnp.arange(seq_len)[None, :] == (lens - 1)[:, None]
    last_idx = (lens - 1)[:, None, None]
    x_last = jnp.take_along_axis(x_norm, last_idx, axis=1)[:, 0]
    h_last = jnp.take_along_axis(hidden, last_idx, axis=1)[:, 0].astype(jnp.float32)
    q_raw = jnp.dot(x_last, w_q, preferred_element_type=jnp.float32).astype(jnp.bfloat16)
    attn_out, attn_pull = jax.vjp(functools.partial(attend, lens=lens), q_raw, k_raw, v_raw, g_q, g_k)
    h_mid = h_last + lax.psum(jnp.dot(attn_out, w_o, preferred_element_type=jnp.float32), 'tp')
    y_norm = norm_rows(h_mid, g_post).astype(jnp.bfloat16)
    gate_val = jnp.dot(y_norm, w_gate, preferred_element_type=jnp.float32).astype(jnp.bfloat16)
    up_val = jnp.dot(y_norm, w_up, preferred_element_type=jnp.float32).astype(jnp.bfloat16)
    hidden_act, act_pull = jax.vjp(swiglu, gate_val.astype(jnp.float32), up_val.astype(jnp.float32))
    hidden_act = hidden_act.astype(jnp.bfloat16)
    h_out = h_mid + lax.psum(jnp.dot(hidden_act, w_down, preferred_element_type=jnp.float32), 'tp')
    emb_out, head_pull = jax.vjp(final_head, h_out, g_final)
    saved = (hidden, x_norm, at_last, x_last, attn_out, attn_pull, h_mid, y_norm, act_pull, hidden_act, head_pull)
    return emb_out, saved


def embed_bwd(saved, d_emb, weights):
    w_q, w_k, w_v, w_o, w_gate, w_up, w_down, g_in, g_q, g_k, g_post, g_final = weights
    hidden, x_norm, at_last, x_last, attn_out, attn_pull, h_mid, y_norm, act_pull, hidden_act, head_pull = saved
    d_hout, d_gfinal = head_pull(d_emb)
    d_hout_b = d_hout.astype(jnp.bfloat16)
    d_act = jnp.einsum('nd,fd->nf', d_hout_b, w_down, preferred_element_type=jnp.float32).astype(jnp.bfloat16)
    d_wdown = jnp.einsum('nf,nd->fd', hidden_act, d_hout_b, preferred_element_type=jnp.float32)
    d_gate, d_up = act_pull(d_act.astype(jnp.float32))
    d_gate = d_gate.astype(jnp.bfloat16)
    d_up = d_up.astype(jnp.bfloat16)
    d_wgate = jnp.einsum('nd,nf->df', y_norm, d_gate, preferred_element_type=jnp.float32)
    d_wup = jnp.einsum('nd,nf->df', y_norm, d_up, preferred_element_type=jnp.float32)
    d_y = lax.psum(jnp.einsum('nf,df->nd', d_gate, w_gate, preferred_element_type=jnp.float32) + jnp.einsum('nf,df->nd', d_up, w_up, preferred_element_type=jnp.float32), 'tp')
    d_ymid, d_gpost = norm_back(h_mid, g_post, d_y)
    d_hmid = d_hout + d_ymid
    d_hmid_b = d_hmid.astype(jnp.bfloat16)
    d_attn = jnp.einsum('nd,ed->ne', d_hmid_b, w_o, preferred_element_type=jnp.float32).astype(jnp.bfloat16)
    d_wo = jnp.einsum('ne,nd->ed', attn_out, d_hmid_b, preferred_element_type=jnp.float32)
    d_qraw, d_kraw, d_vraw, d_gq, d_gk = attn_pull(d_attn)
    d_wq = jnp.einsum('nd,ne->de', x_last, d_qraw, preferred_element_type=jnp.float32)
    d_wk = jnp.einsum('nsd,nse->de', x_norm, d_kraw, preferred_element_type=jnp.float32)
    d_wv = jnp.einsum('nsd,nse->de', x_norm, d_vraw, preferred_element_type=jnp.float32)
    d_xlast = jnp.einsum('ne,de->nd', d_qraw, w_q, preferred_element_type=jnp.float32)
    d_x = jnp.einsum('nse,de->nsd', d_kraw, w_k, preferred_element_type=jnp.float32) + jnp.einsum('nse,de->nsd', d_vraw, w_v, preferred_element_type=jnp.float32)
    d_x = lax.psum(jnp.where(at_last[:, :, None], d_x + d_xlast[:, None, :], d_x), 'tp')
    d_hid, d_gin = norm_back(hidden.astype(jnp.float32), g_in, d_x)
    d_hid = jnp.where(at_last[:, :, None], d_hid + d_hmid[:, None, :], d_hid)
    return d_hid.astype(jnp.bfloat16), (d_wq, d_wk, d_wv, d_wo, d_wgate, d_wup, d_wdown, d_gin, d_gq, d_gk, d_gpost, d_gfinal)


def solution(mesh):
    dp_size = mesh.shape['dp']

    def device_step(hid_q, hid_d, len_q, len_d, pos_doc, w_q, w_k, w_v, w_o, w_gate, w_up, w_down, g_in, g_q, g_k, g_post, g_final):
        weights = (w_q, w_k, w_v, w_o, w_gate, w_up, w_down) + tuple(gain_vec.astype(jnp.float32) for gain_vec in (g_in, g_q, g_k, g_post, g_final))
        n_query = hid_q.shape[0] * dp_size
        emb_q, saved_q = embed_fwd(hid_q, len_q, weights)
        emb_d, saved_d = embed_fwd(hid_d, len_d, weights)
        all_docs = lax.all_gather(emb_d, 'dp', axis=0, tiled=True)
        logits = jnp.einsum('qd,kd->qk', emb_q, all_docs, precision=lax.Precision.HIGHEST) / value_a11
        log_norm = jax.nn.logsumexp(logits, axis=1)
        is_pos = jnp.arange(all_docs.shape[0])[None, :] == pos_doc[:, None]
        pos_logit = jnp.sum(jnp.where(is_pos, logits, 0.0), axis=1)
        loss_rows = log_norm - pos_logit
        d_logits = (jnp.exp(logits - log_norm[:, None]) - is_pos.astype(jnp.float32)) / (n_query * value_a11)
        d_emb_q = jnp.einsum('qk,kd->qd', d_logits, all_docs, precision=lax.Precision.HIGHEST)
        d_docs = jnp.einsum('qk,qd->kd', d_logits, emb_q, precision=lax.Precision.HIGHEST)
        d_emb_d = lax.psum_scatter(d_docs, 'dp', scatter_dimension=0, tiled=True)
        d_hid_q, grads_q = embed_bwd(saved_q, d_emb_q, weights)
        d_hid_d, grads_d = embed_bwd(saved_d, d_emb_d, weights)
        grads = [grad_a + grad_b for grad_a, grad_b in zip(grads_q, grads_d)]
        head_grads = lax.psum((grads[8], grads[9]), ('tp', 'dp'))
        dp_grads = lax.psum(tuple(grads[:8]) + (grads[10], grads[11]), 'dp')
        return (loss_rows, d_hid_q, d_hid_d) + tuple(dp_grads[:8]) + tuple(head_grads) + tuple(dp_grads[8:])

    col_split = P(None, 'tp')
    row_split = P('tp', None)
    in_specs = (P('dp'), P('dp'), P('dp'), P('dp'), P('dp'), col_split, col_split, col_split, row_split, col_split, col_split, row_split, P(), P(), P(), P(), P())
    out_specs = (P('dp'), P('dp'), P('dp'), col_split, col_split, col_split, row_split, col_split, col_split, row_split, P(), P(), P(), P(), P())
    return jax.shard_map(device_step, mesh=mesh, in_specs=in_specs, out_specs=out_specs, check_vma=False)
```

profile of v0, /device:TPU:0, one launch (start us, length us, event | category | flops | bytes accessed | tf_op | source)
XLA Modules:
  0.0 4957.5 jit_solution(17176858574204924268)
XLA Ops:
  94.0 44.8 fusion.5
  138.8 43.8 convolution_convert_fusion.1
  182.6 45.2 multiply_reduce_fusion.2
  299.3 46.2 copy.129
  345.5 45.0 multiply_multiply_fusion
  390.6 66.4 %subtract_convert_fusion = (bf16[64,512,4,64]{3,1,2,0:T(8,128)(2,1)}, bf16[64,512,4,64]{3,1,2,0:T(8,128)(2,1)}) fusion(f32[64,512,4,128]{3,1,2,0:T(8,128)} %multiply_multiply_fusion, f32[512,64]{1,0:T(8,128)S(1)} %copy-done.21, f32[512,64]{1,0:T(8,128)S(1)} %copy-done.18), kind=kLoop, calls=%fused_computation.31 | loop fusion | flops 67108864 | bytes 100925440 | tf_op jit(solution)/shard_map/convert.8
  457.5 27.1 fusion.123
  725.9 27.3 fusion.40
  879.9 29.4 add_select_fusion.3
  910.3 88.1 %multiply_add_fusion.1 = (f32[64,512,4,64]{3,1,2,0:T(8,128)}, f32[64,512,4,64]{3,1,2,0:T(8,128)}) fusion(f32[64,512,4,128]{3,1,2,0:T(8,128)} %convert_bitcast_fusion, f32[512,64]{1,0:T(8,128)S(1)} %copy-done.22, f32[512,64]{1,0:T(8,128)S(1)} %copy-done.19), kind=kLoop, calls=%fused_computation.29 | loop fusion | flops 58720256 | bytes 134479872 | tf_op jit(solution)/shard_map/transpose(jvp())/add_any | solution.py:30
  998.4 69.0 %multiply_reduce_fusion = (f32[128]{0:T(128)}, f32[64,512,4]{1,2,0:T(4,128)S(1)}) fusion(f32[64,512,4,128]{3,1,2,0:T(8,128)} %copy.129, f32[64,512,4]{1,2,0:T(4,128)S(1)} %copy-done.10, f32[64,512,4,64]{3,1,2,0:T(8,128)} %get-tuple-element.68, f32[64,512,4,64]{3,1,2,0:T(8,128)} %get-tuple-element.67, f32[128]{0:T(128)S(1)} %copy-done.131), kind=kLoop, calls=%fused_computation.25 | loop fusion | flops 117309312 | bytes 135267328 | tf_op jit(solution)/shard_map/transpose(jvp())/reduce_sum | solution.py:13
  1067.7 71.8 %fusion.11 = bf16[64,512,4,128]{3,1,2,0:T(8,128)(2,1)} fusion(f32[64,512,4,128]{3,1,2,0:T(8,128)} %copy.129, f32[64,512,4]{1,2,0:T(4,128)S(1)} %multiply_multiply_fusion.2, f32[128]{0:T(128)S(1)} %copy-done.131, f32[64,512,4]{1,2,0:T(4,128)S(1)} %copy-done.10, f32[64,512,4,64]{3,1,2,0:T(8,128)} %get-tuple-element.68, f32[64,512,4,64]{3,1,2,0:T(8,128)} %get-tuple-element.67), kind=kLoop, calls=%fused_computation.23 | loop fusion | flops 117440512 | bytes 168821248 | tf_op jit(solution)/shard_map/transpose(jvp())/convert_element_type | solution.py:40
  1139.6 44.6 copy.145
  1199.8 60.7 %fusion.53 = f32[64,512,1024]{2,1,0:T(8,128)} fusion(bf16[64,512,512]{1,2,0:T(8,128)(2,1)} %bitcast.201, bf16[1024,512]{1,0:T(8,128)(2,1)S(1)} %copy-done.174), kind=kOutput, calls=%fused_computation.127 | convolution fusion | flops 34359738368 | bytes 168820736 | tf_op jit(solution)/shard_map/nse,de->nsd/dot_general | solution.py:110
  1260.5 113.9 %add_select_fusion.1 = f32[64,512,1024]{2,1,0:T(8,128)} fusion(f32[64,512,1024]{2,1,0:T(8,128)} %fusion.53, f32[64,1024]{1,0:T(8,128)S(1)} %copy-done.106, pred[64,512]{1,0:T(8,128)(4,1)S(1)} %copy-done.111, bf16[64,512,512]{1,2,0:T(8,128)(2,1)} %bitcast.198, bf16[1024,512]{1,0:T(8,128)(2,1)S(1)} %copy-done.176), kind=kOutput, calls=%fused_computation.12 | convolution fusion | flops 34460401664 | bytes 303333376 | tf_op jit(solution)/shard_map/nse,de->nsd/dot_general | solution.py:110
  1390.9 32.5 all-reduce.8
  1430.6 43.3 fusion.135
  1490.0 43.3 fusion.134
  1549.5 95.2 %all-reduce.21.cloned.1.call-done = f32[16,512,1024]{2,1,0:T(8,128)} async-done(((f32[16,512,1024]{2,1,0:T(8,128)}), f32[16,512,1024]{2,1,0:T(8,128)}) %all-reduce.21.cloned.1.call-update) | async-done | bytes 33554448 | tf_op jit(solution)/shard_map/psum | solution.py:111
  1688.6 2860.1 %all-reduce.23.cloned.1.call-done = f32[64,512,1024]{2,1,0:T(8,128)} async-done(((f32[64,512,1024]{2,1,0:T(8,128)}), f32[64,512,1024]{2,1,0:T(8,128)}) %all-reduce.23.cloned.1.call-update) | async-done | bytes 134217744 | tf_op jit(solution)/shard_map/psum | solution.py:111
  4548.7 60.6 %fusion.10 = (f32[1024]{0:T(1024)S(1)}, f32[64,512]{1,0:T(8,128)S(1)}) fusion(f32[64,512,1024]{2,1,0:T(8,128)} %all-reduce.23.cloned.1.call-done, bf16[64,512,1024]{2,1,0:T(8,128)(2,1)} %param.22, f32[64,512]{1,0:T(8,128)S(1)} %copy-done.43, f32[1024]{0:T(1024)S(1)} %copy-done.109), kind=kLoop, calls=%fused_computation.21 | loop fusion | flops 234847232 | bytes 201596928 | tf_op jit(solution)/shard_map/reduce_sum | solution.py:20
  4609.4 24.7 all-reduce.9
  4634.1 83.8 %fusion.2 = bf16[64,512,1024]{2,1,0:T(8,128)(2,1)} fusion(bf16[64,512,1024]{2,1,0:T(8,128)(2,1)} %param.22, f32[64,512,1024]{2,1,0:T(8,128)} %all-reduce.23.cloned.1.call-done, f32[64,1024]{1,0:T(8,128)S(1)} %copy-done.28, f32[64,512]{1,0:T(8,128)S(1)} %broadcast_multiply_fusion, f32[64,512]{1,0:T(8,128)S(1)} %copy-done.80, f32[1024]{0:T(1024)S(1)} %copy-done.109, ...), kind=kLoop, calls=%fused_computation.13 | loop fusion | flops 301989888 | bytes 269127680 | tf_op jit(solution)/shard_map/convert_element_type | solution.py:114
  4717.9 207.1 %all-reduce.25.cloned.1.call-done = (f32[1024,1024]{1,0:T(8,128)}, f32[1024,512]{1,0:T(8,128)}, f32[1024,512]{1,0:T(8,128)}, f32[1024,1024]{1,0:T(8,128)}, f32[1...) async-done(((f32[1024,1024]{1,0:T(8,128)}, f32[1024,512]{1,0:T(8,128)}, f32[1024,512]{1,0:T(8,128)}, f32[1024,1024]{1,0:T(8,128)}, ...) | async-done | bytes 31457296 | tf_op jit(solution)/shard_map/psum | solution.py:139
  (571 shorter events, 666.8 us)
Async XLA Ops:
  7.2 538.2 %copy-start = (bf16[1536,1024]{1,0:T(8,128)(2,1)S(1)}, bf16[1536,1024]{1,0:T(8,128)(2,1)}, u32[]{:S(2)}) copy-start(bf16[1536,1024]{1,0:T(8,128)(2,1)} %param.32) | copy-start | bytes 9437188
  7.2 523.0 %all-reduce.31.cloned.1.call-start = ((), (), s32[]{:S(2)}) async-start(), calls=%async_computation.8 | async-start | bytes 655360 | tf_op jit(solution)/shard_map/psum | solution.py:75
  506.7 61.8 %all-reduce.29.cloned.1.call-start = ((), (), s32[]{:S(2)}) async-start(), calls=%async_computation.7 | async-start | bytes 655360 | tf_op jit(solution)/shard_map/psum | solution.py:81
  533.0 79.2 %copy-start.46 = (f32[16,1024]{1,0:T(8,128)}, f32[16,1024]{1,0:T(8,128)S(1)}, u32[]{:S(2)}) copy-start(f32[16,1024]{1,0:T(8,128)S(1)} %get-tuple-element.64) | copy-start | bytes 196612
  547.9 47.2 all-gather.2.cloned.1.call-start
  548.0 162.9 %copy-start.75 = (f32[1024]{0:T(1024)}, f32[1024]{0:T(1024)S(1)}, u32[]{:S(2)}) copy-start(f32[1024]{0:T(1024)S(1)} %convert_element_type.286) | copy-start | bytes 12292
  569.7 141.2 %copy-start.8 = (f32[64,1024]{1,0:T(8,128)}, f32[64,1024]{1,0:T(8,128)S(1)}, u32[]{:S(2)}) copy-start(f32[64,1024]{1,0:T(8,128)S(1)} %get-tuple-element.62) | copy-start | bytes 786436
  571.2 68.7 %reduce-scatter.2.cloned.1.call-start = ((), (), s32[]{:S(2)}) async-start(), calls=%async_computation.3 | async-start | bytes 2359296 | tf_op jit(solution)/shard_map/reduce_scatter | solution.py:134
  604.5 70.0 %all-reduce.27.cloned.1.call-start = ((), (), s32[]{:S(2)}) async-start(), calls=%async_computation.6 | async-start | bytes 655360 | tf_op jit(solution)/shard_map/psum | solution.py:99
  653.9 990.8 %all-reduce.21.cloned.1.call-start = ((), (), s32[]{:S(2)}) async-start(), calls=%async_computation.2 | async-start | bytes 67108864 | tf_op jit(solution)/shard_map/psum | solution.py:111
  909.3 89.1 %copy-start.10 = (f32[64,512,4]{1,2,0:T(4,128)S(1)}, f32[64,512,4]{1,2,0:T(4,128)}, u32[]{:S(2)}) copy-start(f32[64,512,4]{1,2,0:T(4,128)} %fusion.60) | copy-start | bytes 1572868
  909.3 3639.4 %all-reduce.23.cloned.1.call-start = ((), (), s32[]{:S(2)}) async-start(), calls=%async_computation.4 | async-start | bytes 268435456 | tf_op jit(solution)/shard_map/psum | solution.py:111
  1374.4 3550.5 %all-reduce.25.cloned.1.call-start = ((), (), s32[]{:S(2)}) async-start(), calls=%async_computation.5 | async-start | bytes 62914560 | tf_op jit(solution)/shard_map/psum | solution.py:139
  1549.4 95.2 %copy-start.86 = (f32[16,512]{1,0:T(8,128)S(1)}, f32[16,512]{1,0:T(8,128)}, u32[]{:S(2)}) copy-start(f32[16,512]{1,0:T(8,128)} %copy-done.85) | copy-start | bytes 98308
  1549.4 95.2 %copy-start.109 = (f32[1024]{0:T(1024)S(1)}, f32[1024]{0:T(1024)}, u32[]{:S(2)}) copy-start(f32[1024]{0:T(1024)} %copy-done.108) | copy-start | bytes 12292
  1549.5 114.6 %copy-start.65 = (f32[16,1024]{1,0:T(8,128)S(1)}, f32[16,1024]{1,0:T(8,128)}, u32[]{:S(2)}) copy-start(f32[16,1024]{1,0:T(8,128)} %copy-done.63) | copy-start | bytes 196612
  1549.5 114.6 %copy-start.110 = (f32[16,512]{1,0:T(8,128)S(1)}, f32[16,512]{1,0:T(8,128)}, u32[]{:S(2)}) copy-start(f32[16,512]{1,0:T(8,128)} %get-tuple-element.89) | copy-start | bytes 98308
  1549.5 114.6 %copy-start.123 = (pred[16,512]{1,0:T(8,128)(4,1)S(1)}, pred[16,512]{1,0:T(8,128)(4,1)}, u32[]{:S(2)}) copy-start(pred[16,512]{1,0:T(8,128)(4,1)} %iota_compare_fusion.2) | copy-start | bytes 24580
  1664.1 2884.6 %copy-start.43 = (f32[64,512]{1,0:T(8,128)S(1)}, f32[64,512]{1,0:T(8,128)}, u32[]{:S(2)}) copy-start(f32[64,512]{1,0:T(8,128)} %copy-done.42) | copy-start | bytes 393220
  1688.6 2920.8 %copy-start.136 = (f32[1024]{0:T(1024)S(1)}, f32[1024]{0:T(1024)}, u32[]{:S(2)}) copy-start(f32[1024]{0:T(1024)} %add.364) | copy-start | bytes 12292
  1688.6 2920.8 %copy-start.137 = (f32[1024]{0:T(1024)S(1)}, f32[1024]{0:T(1024)}, u32[]{:S(2)}) copy-start(f32[1024]{0:T(1024)} %add.363) | copy-start | bytes 12292
  1688.6 2945.5 %copy-start.28 = (f32[64,1024]{1,0:T(8,128)S(1)}, f32[64,1024]{1,0:T(8,128)}, u32[]{:S(2)}) copy-start(f32[64,1024]{1,0:T(8,128)} %copy-done.26) | copy-start | bytes 786436
  1688.6 2945.5 %copy-start.80 = (f32[64,512]{1,0:T(8,128)S(1)}, f32[64,512]{1,0:T(8,128)}, u32[]{:S(2)}) copy-start(f32[64,512]{1,0:T(8,128)} %get-tuple-element.83) | copy-start | bytes 393220
  1688.6 2945.5 %copy-start.112 = (pred[64,512]{1,0:T(8,128)(4,1)S(1)}, pred[64,512]{1,0:T(8,128)(4,1)}, u32[]{:S(2)}) copy-start(pred[64,512]{1,0:T(8,128)(4,1)} %iota_compare_fusion) | copy-start | bytes 98308
  (169 other events, 3980.8 us)
Sparse Core Ops, SparseCore 0:
  506.9 23.2 all-reduce.30
  548.0 20.4 all-reduce.28
  571.4 23.7 all-gather.1
  604.7 35.2 reduce-scatter.1
  654.0 20.4 all-reduce.26
  909.4 735.1 all-reduce.20
  1647.1 2901.5 all-reduce.22
  4555.0 369.9 all-reduce.24
where the time goes:
time: 4970 us; the launch traced here: 4960 us
  waiting for transfers between devices  3260 us (66%)
  other arithmetic  753 us (15%)
  matrix products  708 us (14%)
  local copies, waits for them, and re-layouts  162 us (3%)
  blocking collectives  57.2 us (1%)
    psum x2, waiting for transfers between devices, embed_bwd(): lax.psum(jnp.where(at_last[:, :, None], d_x + d_xlast[:, None, :], d_x),...  2960 us
    psum x1, waiting for transfers between devices, device_step(): dp_grads = lax.psum(tuple(grads[:8]) + (grads[10], grads[11]), 'dp')  207 us
    dot_general x2, matrix products, embed_bwd(): jnp.einsum('nse,de->nsd', d_vraw, w_v, preferred_element_type=jnp.float32)  143 us
    convert_element_type x4, local copies, waits for them, and re-layouts, attend(): k_raw.reshape(n_seq, seq_len, n_kv, head_dim).astype(jnp.float32)  116 us
    convert_element_type x2, other arithmetic, embed_bwd(): d_hid.astype(jnp.bfloat16)  108 us
    add_any x4, other arithmetic, rotate(): second_half * sin_a  107 us
  transfers between devices with their start and end apart: 8, of which 8 were waited for; matrix products, arithmetic and copies ran while one was open for 16% of the time, Pallas kernels for 0%

commit v1 on v0

v1 whole, which is shorter than its diff:
```python
import functools
import jax
import jax.numpy as jnp
from jax import lax
from jax.experimental import pallas as pl
from jax.experimental.pallas import tpu as pltpu
from jax.sharding import PartitionSpec as P

NORM_EPS = 1e-6
ROPE_THETA = 1000000.0
TEMPERATURE = 0.05
HEAD = 128
MAX_QUERY_LEN = 128
F32 = jnp.float32
BF16 = jnp.bfloat16
NT = (((1,), (1,)), ((), ()))
TN = (((0,), (0,)), ((), ()))
NN = (((1,), (0,)), ((), ()))


def mm(lhs, rhs, dims):
    return lax.dot_general(lhs, rhs, dims, preferred_element_type=F32)


def norm_rows(values, gain_vec):
    return values * lax.rsqrt(jnp.mean(values * values, axis=-1, keepdims=True) + NORM_EPS) * gain_vec


def norm_back(values, gain_vec, d_out):
    scale = lax.rsqrt(jnp.mean(values * values, axis=-1, keepdims=True) + NORM_EPS)
    g_dout = d_out * gain_vec
    d_values = scale * g_dout - values * scale ** 3 * jnp.mean(values * g_dout, axis=-1, keepdims=True)
    d_gain = jnp.sum((d_out * values * scale).reshape(-1, values.shape[-1]), axis=0)
    return d_values, d_gain


def rotate(values, angles):
    half_dim = values.shape[-1] // 2
    first_half = values[..., :half_dim]
    second_half = values[..., half_dim:]
    cos_a = jnp.cos(angles)
    sin_a = jnp.sin(angles)
    return jnp.concatenate([first_half * cos_a - second_half * sin_a, second_half * cos_a + first_half * sin_a], axis=-1)


def final_head(h_out, g_final):
    z_norm = norm_rows(h_out, g_final)
    return z_norm * lax.rsqrt(jnp.sum(z_norm * z_norm, axis=-1, keepdims=True))


def swiglu(gate_in, up_in):
    return jax.nn.silu(gate_in) * up_in


def block_queries(q_heads, n_kv):
    n_heads = q_heads.shape[0]
    wide = jnp.concatenate([q_heads] * n_kv, axis=1)
    row = lax.broadcasted_iota(jnp.int32, wide.shape, 0)
    col = lax.broadcasted_iota(jnp.int32, wide.shape, 1)
    return jnp.where(col // HEAD == row // (n_heads // n_kv), wide, 0.0).astype(BF16)


def norm_chunk(h_ref, gin_ref, x_scr, r_scr, start, chunk):
    sub = 32
    for blk in range(chunk // sub):
        rows = pl.ds(pl.multiple_of(start + blk * sub, sub), sub)
        h = h_ref[0, rows, :].astype(F32)
        scale = lax.rsqrt(jnp.mean(h * h, axis=-1, keepdims=True) + NORM_EPS)
        x_scr[rows, :] = (h * scale * gin_ref[...]).astype(BF16)
        if r_scr is not None:
            r_scr[rows, :] = scale


def rotate_keys(k_b, gk, cos, sin):
    k_f = k_b.astype(F32)
    scale = lax.rsqrt(jnp.sum(k_f * k_f, axis=0, keepdims=True) * (1.0 / HEAD) + NORM_EPS)
    k_n = k_f * scale * gk
    half = HEAD // 2
    k1, k2 = k_n[:half], k_n[half:]
    rot = jnp.concatenate([k1 * cos - k2 * sin, k2 * cos + k1 * sin], axis=0)
    return rot.astype(BF16), scale


def fwd_kernel(len_ref, h_ref, wk_ref, q_ref, gin_ref, gk_ref, cos_ref, sin_ref, u_ref, x_scr, kr_scr, s_scr, *, chunk, n_chunk, n_kv):
    length = len_ref[pl.program_id(0)]
    n_heads = q_ref.shape[1]
    q_wide = block_queries(q_ref[0], n_kv)
    s_scr[...] = jnp.full(s_scr.shape, -1e30, F32)
    n_live = (length + chunk - 1) // chunk

    def score(c, carry):
        start = pl.multiple_of(c * chunk, chunk)
        norm_chunk(h_ref, gin_ref, x_scr, None, start, chunk)
        x = x_scr[pl.ds(start, chunk), :]
        for pair in range(n_kv // 2):
            k_pair = mm(wk_ref[pair * 2 * HEAD:(pair + 1) * 2 * HEAD, :], x, NT).astype(BF16)
            for j in range(2):
                for lane in range(chunk // 128):
                    lanes = slice(lane * 128, (lane + 1) * 128)
                    rot, _ = rotate_keys(k_pair[j * HEAD:(j + 1) * HEAD, lanes], gk_ref[...], cos_ref[c, :, lanes], sin_ref[c, :, lanes])
                    base = (pair * 2 + j) * HEAD
                    kr_scr[base:base + HEAD, lanes] = rot
        scores = mm(q_wide, kr_scr[...], NN) * HEAD ** -0.5
        at = start + lax.broadcasted_iota(jnp.int32, scores.shape, 1)
        s_scr[c] = jnp.where(at < length, scores, -1e30)
        return carry

    lax.fori_loop(0, n_live, score, 0)
    s_all = s_scr[...]
    top = jnp.max(jnp.max(s_all, axis=0), axis=-1, keepdims=True)
    p_all = jnp.exp(s_all - top[None])
    total = jnp.sum(jnp.sum(p_all, axis=0), axis=-1, keepdims=True)
    s_scr[...] = p_all / total[None]
    u_ref[0] = jnp.zeros((n_heads, u_ref.shape[2]), F32)

    def mix(c, carry):
        start = pl.multiple_of(c * chunk, chunk)
        u_ref[0] += mm(s_scr[c].astype(BF16), x_scr[pl.ds(start, chunk), :], NN)
        return carry

    lax.fori_loop(0, n_live, mix, 0)


def bwd_kernel(len_ref, tp_ref, h_ref, wk_ref, q_ref, gv_ref, gin_ref, gk_ref, cos_ref, sin_ref,
               dh_ref, dw_ref, dgk_ref, dgin_ref, dq_ref, dxl_ref,
               w_scr, x_scr, r_scr, k_scr, kr_scr, rk_scr, s_scr, dp_scr, dk_scr, dx_scr, *, chunk, n_chunk, n_kv):
    length = len_ref[pl.program_id(0)]
    n_heads = q_ref.shape[1]
    kv_width = n_kv * HEAD
    half_kv = kv_width // 2
    half = HEAD // 2
    q_wide = block_queries(q_ref[0], n_kv)
    n_live = (length + chunk - 1) // chunk

    @pl.when(pl.program_id(0) == 0)
    def _():
        w_scr[:kv_width, :] = wk_ref[...].astype(BF16)
        dw_ref[...] = jnp.zeros(dw_ref.shape, F32)
        dgk_ref[...] = jnp.zeros(dgk_ref.shape, F32)
        dgin_ref[...] = jnp.zeros(dgin_ref.shape, F32)

    w_scr[kv_width:, :] = gv_ref[0].astype(BF16)
    s_scr[...] = jnp.full(s_scr.shape, -1e30, F32)
    dp_scr[...] = jnp.zeros(dp_scr.shape, F32)

    def score(c, carry):
        start = pl.multiple_of(c * chunk, chunk)
        norm_chunk(h_ref, gin_ref, x_scr, r_scr, start, chunk)
        x = x_scr[pl.ds(start, chunk), :]
        for pair in range(n_kv // 2):
            low = pair * 2 * HEAD
            high = low + 2 * HEAD if pair < n_kv // 2 - 1 else kv_width + n_heads
            prod = mm(w_scr[low:high, :], x, NT)
            if pair == n_kv // 2 - 1:
                dp_scr[c] = prod[2 * HEAD:]
            k_pair = prod[:2 * HEAD].astype(BF16)
            k_scr[c, low:low + 2 * HEAD, :] = k_pair
            for j in range(2):
                for lane in range(chunk // 128):
                    lanes = slice(lane * 128, (lane + 1) * 128)
                    rot, scale = rotate_keys(k_pair[j * HEAD:(j + 1) * HEAD, lanes], gk_ref[...], cos_ref[c, :, lanes], sin_ref[c, :, lanes])
                    head = pair * 2 + j
                    kr_scr[c, head * HEAD:(head + 1) * HEAD, lanes] = rot
                    rk_scr[c, head:head + 1, lanes] = scale
        scores = mm(q_wide, kr_scr[c], NN) * HEAD ** -0.5
        at = start + lax.broadcasted_iota(jnp.int32, scores.shape, 1)
        s_scr[c] = jnp.where(at < length, scores, -1e30)
        return carry

    lax.fori_loop(0, n_live, score, 0)
    s_all = s_scr[...]
    top = jnp.max(jnp.max(s_all, axis=0), axis=-1, keepdims=True)
    p_all = jnp.exp(s_all - top[None])
    total = jnp.sum(jnp.sum(p_all, axis=0), axis=-1, keepdims=True)
    p_all = p_all / total[None]
    dp_all = dp_scr[...]
    mean_dp = jnp.sum(jnp.sum(p_all * dp_all, axis=0), axis=-1, keepdims=True)
    s_scr[...] = p_all
    dp_scr[...] = p_all * (dp_all - mean_dp[None]) * HEAD ** -0.5
    dq_ref[0] = jnp.zeros(dq_ref.shape[1:], F32)

    def back(c, carry):
        start = pl.multiple_of(c * chunk, chunk)
        ds_b = dp_scr[c].astype(BF16)
        dk_scr[kv_width:, :] = s_scr[c].astype(BF16)
        dq_ref[0] += mm(ds_b, kr_scr[c], NT)
        gk = gk_ref[...]
        for head in range(n_kv):
            d_rot = mm(q_wide[:, head * HEAD:(head + 1) * HEAD], ds_b, TN)
            for lane in range(chunk // 128):
                lanes = slice(lane * 128, (lane + 1) * 128)
                cos, sin = cos_ref[c, :, lanes], sin_ref[c, :, lanes]
                d1, d2 = d_rot[:half, lanes], d_rot[half:, lanes]
                d_n = jnp.concatenate([d1 * cos + d2 * sin, d2 * cos - d1 * sin], axis=0)
                k_f = k_scr[c, head * HEAD:(head + 1) * HEAD, lanes].astype(F32)
                scale = rk_scr[c, head:head + 1, lanes]
                prod = k_f * d_n
                dgk_ref[...] += prod * scale
                inner = jnp.sum(prod * gk, axis=0, keepdims=True) * (1.0 / HEAD)
                d_k = d_n * gk * scale - k_f * (scale * scale * scale * inner)
                dk_scr[head * HEAD:(head + 1) * HEAD, lanes] = d_k.astype(BF16)
        x = x_scr[pl.ds(start, chunk), :]
        own = pl.multiple_of(tp_ref[0] * half_kv, half_kv)
        dw_ref[...] += mm(dk_scr[pl.ds(own, half_kv), :], x, NN)
        dx_scr[...] = mm(dk_scr[...], w_scr[...], TN)
        sub = 32
        gin = gin_ref[...]
        for blk in range(chunk // sub):
            here = slice(blk * sub, (blk + 1) * sub)
            rows = pl.ds(pl.multiple_of(start + blk * sub, sub), sub)
            h = h_ref[0, rows, :].astype(F32)
            scale = r_scr[rows, :]
            d_x = dx_scr[here, :]
            g_dx = d_x * gin
            inner = jnp.mean(h * g_dx, axis=-1, keepdims=True)
            dh_ref[0, rows, :] = (scale * g_dx - h * (scale * scale * scale * inner)).astype(BF16)
            dgin_ref[...] += jnp.sum((d_x * h * scale).reshape(sub // 8, 8, h.shape[1]), axis=0)

        @pl.when((length - 1) // chunk == c)
        def _():
            dxl_ref[0] = dx_scr[pl.ds(length - 1 - start, 1), :]

        return carry

    lax.fori_loop(0, n_live, back, 0)
    for c in range(1, n_chunk):
        @pl.when(c >= n_live)
        def _():
            dh_ref[0, c * chunk:(c + 1) * chunk, :] = jnp.zeros((chunk, dh_ref.shape[2]), BF16)
    tail = dh_ref.shape[1] - n_chunk * chunk
    if tail:
        dh_ref[0, n_chunk * chunk:, :] = jnp.zeros((tail, dh_ref.shape[2]), BF16)


def outer_kernel(a_ref, b_ref, o_ref):
    o_ref[...] = mm(a_ref[...].astype(BF16), b_ref[...].astype(BF16), TN)


def outer_sum(rows_a, at_a, rows_b, n_cols):
    n_rows, width = rows_b.shape
    block = min(256, width)
    return pl.pallas_call(
        outer_kernel,
        grid=(width // block,),
        in_specs=[pl.BlockSpec((n_rows, n_cols), lambda i: (0, at_a)), pl.BlockSpec((n_rows, block), lambda i: (0, i))],
        out_specs=pl.BlockSpec((n_cols, block), lambda i: (0, i)),
        out_shape=jax.ShapeDtypeStruct((n_cols, width), F32),
        cost_estimate=pl.CostEstimate(flops=2 * n_rows * n_cols * width, bytes_accessed=4 * n_rows * (n_cols + width), transcendentals=0),
        name="outer_sum",
    )(rows_a, rows_b)


def value_kernel(d_ref, w_ref, o_ref):
    o_ref[...] = mm(d_ref[...].astype(BF16), w_ref[0].astype(BF16), NN)


def value_rows(d_heads, wv_heads, group):
    n_seq, total = d_heads.shape
    n_heads, width = total // HEAD, wv_heads.shape[2]
    out = pl.pallas_call(
        value_kernel,
        grid=(n_heads,),
        in_specs=[pl.BlockSpec((n_seq, HEAD), lambda i: (0, i)), pl.BlockSpec((1, HEAD, width), lambda i: (i // group, 0, 0))],
        out_specs=pl.BlockSpec((n_seq, width), lambda i: (0, i)),
        out_shape=jax.ShapeDtypeStruct((n_seq, n_heads * width), F32),
        cost_estimate=pl.CostEstimate(flops=2 * n_seq * total * width, bytes_accessed=4 * n_seq * n_heads * width, transcendentals=0),
        name="value_rows",
    )(d_heads, wv_heads)
    return out.reshape(n_seq, n_heads, width)


def rope_tables(n_chunk, chunk):
    inv_freq = ROPE_THETA ** (-jnp.arange(0, HEAD, 2, dtype=F32) / HEAD)
    angle = inv_freq[:, None] * jnp.arange(n_chunk * chunk, dtype=F32)[None, :]
    split = lambda t: t.reshape(HEAD // 2, n_chunk, chunk).transpose(1, 0, 2)
    return split(jnp.cos(angle)), split(jnp.sin(angle))


def whole(shape):
    return pl.BlockSpec(shape, lambda *_: (0,) * len(shape))


def per_seq(shape):
    return pl.BlockSpec((1,) + shape, lambda i, *_: (i,) + (0,) * len(shape))


def run_forward(hidden, lens, wk_t, q_heads, g_in, g_k, span, chunk):
    n_seq, _, width = hidden.shape
    n_heads = q_heads.shape[1]
    kv_width = wk_t.shape[0]
    n_chunk = span // chunk
    cos, sin = rope_tables(n_chunk, chunk)
    gk = jnp.broadcast_to(g_k[:, None], (HEAD, 128))
    tokens = n_seq * span
    return pl.pallas_call(
        functools.partial(fwd_kernel, chunk=chunk, n_chunk=n_chunk, n_kv=kv_width // HEAD),
        grid_spec=pltpu.PrefetchScalarGridSpec(
            num_scalar_prefetch=1,
            grid=(n_seq,),
            in_specs=[per_seq((span, width)), whole(wk_t.shape), per_seq((n_heads, HEAD)), whole((1, width)), whole(gk.shape), whole(cos.shape), whole(sin.shape)],
            out_specs=per_seq((n_heads, width)),
            scratch_shapes=[pltpu.VMEM((span, width), BF16), pltpu.VMEM((kv_width, chunk), BF16), pltpu.VMEM((n_chunk, n_heads, chunk), F32)],
        ),
        out_shape=jax.ShapeDtypeStruct((n_seq, n_heads, width), F32),
        compiler_params=pltpu.CompilerParams(dimension_semantics=("arbitrary",), vmem_limit_bytes=56 * 1024 * 1024),
        cost_estimate=pl.CostEstimate(flops=2 * tokens * width * kv_width, bytes_accessed=2 * tokens * width, transcendentals=0),
        name="attend_forward",
    )(lens, hidden, wk_t, q_heads, g_in[None, :], gk, cos, sin)


def run_backward(hidden, lens, tp_index, wk_all, q_heads, g_val, g_in, g_k, span, chunk):
    n_seq, seq_len, width = hidden.shape
    n_heads = q_heads.shape[1]
    kv_width = wk_all.shape[0]
    n_kv = kv_width // HEAD
    n_chunk = span // chunk
    cos, sin = rope_tables(n_chunk, chunk)
    gk = jnp.broadcast_to(g_k[:, None], (HEAD, 128))
    tokens = n_seq * span
    sds = jax.ShapeDtypeStruct
    return pl.pallas_call(
        functools.partial(bwd_kernel, chunk=chunk, n_chunk=n_chunk, n_kv=n_kv),
        grid_spec=pltpu.PrefetchScalarGridSpec(
            num_scalar_prefetch=2,
            grid=(n_seq,),
            in_specs=[per_seq((span, width)), whole(wk_all.shape), per_seq((n_heads, HEAD)), per_seq((n_heads, width)), whole((1, width)), whole(gk.shape), whole(cos.shape), whole(sin.shape)],
            out_specs=[per_seq((seq_len, width)), whole((kv_width // 2, width)), whole((HEAD, 128)), whole((8, width)), per_seq((n_heads, kv_width)), per_seq((1, width))],
            scratch_shapes=[
                pltpu.VMEM((kv_width + n_heads, width), BF16),
                pltpu.VMEM((span, width), BF16),
                pltpu.VMEM((span, 1), F32),
                pltpu.VMEM((n_chunk, kv_width, chunk), BF16),
                pltpu.VMEM((n_chunk, kv_width, chunk), BF16),
                pltpu.VMEM((n_chunk, n_kv, chunk), F32),
                pltpu.VMEM((n_chunk, n_heads, chunk), F32),
                pltpu.VMEM((n_chunk, n_heads, chunk), F32),
                pltpu.VMEM((kv_width + n_heads, chunk), BF16),
                pltpu.VMEM((chunk, width), F32),
            ],
        ),
        out_shape=[sds((n_seq, seq_len, width), BF16), sds((kv_width // 2, width), F32), sds((HEAD, 128), F32), sds((8, width), F32), sds((n_seq, n_heads, kv_width), F32), sds((n_seq, 1, width), F32)],
        compiler_params=pltpu.CompilerParams(dimension_semantics=("arbitrary",), vmem_limit_bytes=56 * 1024 * 1024),
        cost_estimate=pl.CostEstimate(flops=5 * tokens * width * kv_width, bytes_accessed=4 * tokens * width, transcendentals=0),
        name="attend_backward",
    )(lens, tp_index, hidden, wk_all, q_heads, g_val, g_in[None, :], gk, cos, sin)


def patch_kernel(len_ref, rows_ref, src_ref, dst_ref, tiles, sem_in, sem_out, *, n_seq, tile):
    def place(i):
        at = pl.multiple_of(((len_ref[i] - 1) // tile) * tile, tile)
        return src_ref.at[i, pl.ds(at, tile), :], dst_ref.at[i, pl.ds(at, tile), :]

    def fetch(i, carry):
        pltpu.make_async_copy(place(i)[0], tiles.at[i], sem_in.at[i]).start()
        return carry

    def change(i, carry):
        source, target = place(i)
        pltpu.make_async_copy(source, tiles.at[i], sem_in.at[i]).wait()
        row = lax.broadcasted_iota(jnp.int32, tiles.shape[1:], 0)
        new = jnp.broadcast_to(rows_ref[i], tiles.shape[1:])
        tiles[i] = jnp.where(row == (len_ref[i] - 1) % tile, new, tiles[i].astype(F32)).astype(BF16)
        pltpu.make_async_copy(tiles.at[i], target, sem_out.at[i]).start()
        return carry

    def drain(i, carry):
        pltpu.make_async_copy(tiles.at[i], place(i)[1], sem_out.at[i]).wait()
        return carry

    lax.fori_loop(0, n_seq, fetch, 0)
    lax.fori_loop(0, n_seq, change, 0)
    lax.fori_loop(0, n_seq, drain, 0)


def patch_rows(d_hidden, lens, rows):
    n_seq, _, width = d_hidden.shape
    tile = 16
    return pl.pallas_call(
        functools.partial(patch_kernel, n_seq=n_seq, tile=tile),
        in_specs=[pl.BlockSpec(memory_space=pltpu.SMEM), pl.BlockSpec(memory_space=pltpu.VMEM), pl.BlockSpec(memory_space=pl.ANY)],
        out_specs=pl.BlockSpec(memory_space=pl.ANY),
        scratch_shapes=[pltpu.VMEM((n_seq, tile, width), BF16), pltpu.SemaphoreType.DMA((n_seq,)), pltpu.SemaphoreType.DMA((n_seq,))],
        out_shape=jax.ShapeDtypeStruct(d_hidden.shape, BF16),
        input_output_aliases={2: 0},
        name="patch_last_rows",
    )(lens, rows[:, None, :], d_hidden)


def solution(mesh):
    dp_size = mesh.shape['dp']
    tp_size = mesh.shape['tp']
    swap = [(i, (i + 1) % tp_size) for i in range(tp_size)]

    def tp_sum(value):
        return value + lax.ppermute(value, 'tp', swap)

    def device_step(hid_q, hid_d, len_q, len_d, pos_doc, w_q, w_k, w_v, w_o, w_gate, w_up, w_down, g_in, g_q, g_k, g_post, g_final):
        g_in, g_q, g_k, g_post, g_final = (g.astype(F32) for g in (g_in, g_q, g_k, g_post, g_final))
        n_q, n_d = hid_q.shape[0], hid_d.shape[0]
        n_own = n_q + n_d
        width = hid_q.shape[2]
        n_kv = w_k.shape[1] // HEAD
        n_heads = w_q.shape[1] // HEAD
        group = n_heads // n_kv
        tp_i = lax.axis_index('tp')
        dp_i = lax.axis_index('dp')
        span_q, span_d = min(MAX_QUERY_LEN, hid_q.shape[1]), hid_d.shape[1]
        n_query = n_q * dp_size

        wk_t, wv_t = w_k.T, w_v.T
        kv_all = lax.all_gather(jnp.stack([wk_t, wv_t]).astype(F32)[None], 'tp', axis=0, tiled=True)
        wk_all = kv_all[:, 0].reshape(-1, width)
        wv_all = kv_all[:, 1].reshape(tp_size * n_kv, HEAD, width)

        lens = jnp.concatenate([len_q, len_d])
        h_last = jnp.concatenate([
            jnp.take_along_axis(hid, (ln - 1)[:, None, None], axis=1)[:, 0] for hid, ln in ((hid_q, len_q), (hid_d, len_d))
        ]).astype(F32)
        x_last = lax.reduce_precision(norm_rows(h_last, g_in), 8, 7)
        q_raw = mm(x_last.astype(BF16), w_q, NN).astype(BF16)
        inv_freq = ROPE_THETA ** (-jnp.arange(0, HEAD, 2, dtype=F32) / HEAD)
        q_angle = (lens - 1).astype(F32)[:, None, None] * inv_freq

        def rotate_query(raw, gain):
            return rotate(norm_rows(raw, gain), q_angle)

        q_rot, q_pull = jax.vjp(rotate_query, q_raw.astype(F32).reshape(n_own, n_heads, HEAD), g_q)
        q_rot = lax.reduce_precision(q_rot, 8, 7)
        q_all = lax.all_gather(q_rot, 'tp', axis=1, tiled=True)

        u = jnp.concatenate([
            run_forward(hid_q, len_q, wk_t, q_rot[:n_q], g_in, g_k, span_q, min(128, span_q)),
            run_forward(hid_d, len_d, wk_t, q_rot[n_q:], g_in, g_k, span_d, min(256, span_d)),
        ])
        u_b = u.astype(BF16).reshape(n_own, n_kv, group, width)
        wv_heads = w_v.reshape(width, n_kv, HEAD)
        attn_out = jnp.einsum('nkgd,dke->nkge', u_b, wv_heads, preferred_element_type=F32).reshape(n_own, -1)
        attn_out = lax.reduce_precision(attn_out, 8, 7)
        h_mid = h_last + tp_sum(mm(attn_out.astype(BF16), w_o, NN))

        def gate_up(rows):
            y = norm_rows(rows, g_post).astype(BF16)
            return y, mm(y, w_gate, NN).astype(BF16), mm(y, w_up, NN).astype(BF16)

        _, gate_own, up_own = gate_up(h_mid)
        act_own = swiglu(gate_own.astype(F32), up_own.astype(F32)).astype(BF16)
        h_out = h_mid + tp_sum(mm(act_own, w_down, NN))

        note = jnp.zeros((8, 2 * width), F32).at[0, :n_q].set(pos_doc.astype(F32))
        rows_all = lax.all_gather(jnp.concatenate([jnp.concatenate([h_mid, h_out], axis=1), note]), 'dp', axis=0, tiled=False)
        side_all = lax.all_gather(jnp.concatenate([x_last, attn_out], axis=1), 'dp', axis=0, tiled=True)
        pos_all = rows_all[:, n_own, :n_q].reshape(-1).astype(jnp.int32)
        seq_rows = jnp.concatenate([rows_all[:, :n_q].reshape(-1, 2 * width), rows_all[:, n_q:n_own].reshape(-1, 2 * width)])
        mid_all, out_all = seq_rows[:, :width], seq_rows[:, width:]

        emb_all, head_pull = jax.vjp(final_head, out_all, g_final)
        emb_q, emb_d = emb_all[:n_query], emb_all[n_query:]
        logits = jnp.einsum('qd,kd->qk', emb_q, emb_d, precision=lax.Precision.HIGHEST) / TEMPERATURE
        log_norm = jax.nn.logsumexp(logits, axis=1)
        is_pos = jnp.arange(emb_d.shape[0])[None, :] == pos_all[:, None]
        loss_all = log_norm - jnp.sum(jnp.where(is_pos, logits, 0.0), axis=1)
        loss_rows = lax.dynamic_slice_in_dim(loss_all, dp_i * n_q, n_q)
        d_logits = (jnp.exp(logits - log_norm[:, None]) - is_pos.astype(F32)) / (n_query * TEMPERATURE)
        d_emb_q = jnp.einsum('qk,kd->qd', d_logits, emb_d, precision=lax.Precision.HIGHEST)
        d_emb_d = jnp.einsum('qk,qd->kd', d_logits, emb_q, precision=lax.Precision.HIGHEST)
        d_out_all, d_gfinal = head_pull(jnp.concatenate([d_emb_q, d_emb_d]))

        def own_rows(all_rows):
            return jnp.concatenate([
                lax.dynamic_slice_in_dim(all_rows, dp_i * n_q, n_q),
                lax.dynamic_slice_in_dim(all_rows, n_query + dp_i * n_d, n_d),
            ])

        y_all, gate_all, up_all = gate_up(mid_all)
        act_all, act_pull = jax.vjp(swiglu, gate_all.astype(F32), up_all.astype(F32))
        d_out_b = d_out_all.astype(BF16)
        d_act = mm(d_out_b, w_down, NT).astype(BF16)
        d_gate, d_up = (d.astype(BF16) for d in act_pull(d_act.astype(F32)))
        d_wdown = mm(act_all.astype(BF16), d_out_b, TN)
        d_wgate = mm(y_all, d_gate, TN)
        d_wup = mm(y_all, d_up, TN)
        d_y = tp_sum(mm(own_rows(d_gate), w_gate, NT) + mm(own_rows(d_up), w_up, NT))
        d_ymid, d_gpost = norm_back(h_mid, g_post, d_y)
        d_hmid = own_rows(d_out_all) + d_ymid

        d_attn = lax.reduce_precision(mm(d_hmid.astype(BF16), w_o, NT), 8, 7)
        d_attn_all = lax.all_gather(d_attn, 'tp', axis=1, tiled=True)
        g_val = value_rows(d_attn_all, wv_all, group)
        d_wv = jnp.einsum('nkgd,nkge->dke', u_b, d_attn.astype(BF16).reshape(n_own, n_kv, group, HEAD), preferred_element_type=F32).reshape(width, -1)
        d_wv = lax.psum(d_wv, 'dp')
        d_hmid_all = lax.all_gather(d_hmid, 'dp', axis=0, tiled=True)
        d_wo = outer_sum(side_all, 1, d_hmid_all, width)

        tp_arr = tp_i.astype(jnp.int32)[None]
        back_q = run_backward(hid_q, len_q, tp_arr, wk_all, q_all[:n_q], g_val[:n_q], g_in, g_k, span_q, min(128, span_q))
        back_d = run_backward(hid_d, len_d, tp_arr, wk_all, q_all[n_q:], g_val[n_q:], g_in, g_k, span_d, min(256, span_d))
        d_wk_t = back_q[1] + back_d[1]
        d_gk = jnp.sum(back_q[2] + back_d[2], axis=1)
        d_gin = jnp.sum(back_q[3] + back_d[3], axis=0)
        d_rot = jnp.concatenate([back_q[4], back_d[4]]).reshape(n_own, tp_size * n_kv, group, tp_size * n_kv, HEAD)
        d_rot = jnp.sum(jnp.where(jnp.eye(tp_size * n_kv, dtype=bool)[None, :, None, :, None], d_rot, 0.0), axis=3)
        d_rot = lax.dynamic_slice_in_dim(d_rot.reshape(n_own, -1, HEAD), tp_i * n_heads, n_heads, axis=1)
        d_x_row = jnp.concatenate([back_q[5], back_d[5]])[:, 0]

        d_qraw, d_gq = q_pull(d_rot)
        d_qraw = lax.reduce_precision(d_qraw.reshape(n_own, -1), 8, 7)
        gq_row = jnp.zeros((8, width), F32).at[0, :HEAD].set(d_gq)
        both = tp_sum(jnp.concatenate([mm(d_qraw.astype(BF16), w_q, NT), gq_row]))
        d_xlast, d_gq = both[:n_own], both[n_own, :HEAD]
        row_back, _ = norm_back(h_last, g_in, d_x_row + d_xlast)
        d_gin = d_gin + jnp.sum(d_xlast * norm_rows(h_last, 1.0), axis=0)
        last_rows = row_back + d_hmid
        d_hid_q = patch_rows(back_q[0], len_q, last_rows[:n_q])
        d_hid_d = patch_rows(back_d[0], len_d, last_rows[n_q:])

        d_qraw_all = lax.all_gather(d_qraw, 'dp', axis=0, tiled=True)
        d_wq = outer_sum(side_all, 0, d_qraw_all, width)
        gains = jnp.stack([d_gin, d_gpost, jnp.pad(jnp.concatenate([d_gq, d_gk]), (0, width - 2 * HEAD))])
        summed = lax.psum(jnp.concatenate([d_wk_t, jnp.pad(gains, ((0, 5), (0, 0)))]), 'dp')
        n_rows = d_wk_t.shape[0]
        d_wk = summed[:n_rows].T
        d_gin, d_gpost, heads = summed[n_rows], summed[n_rows + 1], summed[n_rows + 2]
        return (loss_rows, d_hid_q, d_hid_d, d_wq, d_wk, d_wv, d_wo, d_wgate, d_wup, d_wdown, d_gin, heads[:HEAD], heads[HEAD:2 * HEAD], d_gpost, d_gfinal)

    col_split = P(None, 'tp')
    row_split = P('tp', None)
    in_specs = (P('dp'), P('dp'), P('dp'), P('dp'), P('dp'), col_split, col_split, col_split, row_split, col_split, col_split, row_split, P(), P(), P(), P(), P())
    out_specs = (P('dp'), P('dp'), P('dp'), col_split, col_split, col_split, row_split, col_split, col_split, row_split, P(), P(), P(), P(), P())
    return jax.shard_map(device_step, mesh=mesh, in_specs=in_specs, out_specs=out_specs, check_vma=False)
```

time: 4970 us -> 1090 us (0.22)
  waiting for transfers between devices: 3260 us -> 259 us
  other arithmetic: 753 us -> 45.3 us
  matrix products: 708 us -> 46.1 us
  Pallas kernels: 0 us -> 637 us
  local copies, waits for them, and re-layouts: 162 us -> 62.1 us
    psum x6 -> x1, waiting for transfers between devices: 3220 us -> 58.6 us  [device_step(): lax.psum(jnp.concatenate([d_wk_t, jnp.pad(gains, ((0, 5), (0, 0)))]), 'dp')]
    pallas_call x0 -> x9, Pallas kernels: none -> 637 us  [the longest x2 451 us: run_backward(): pl.pallas_call(functools.partial(bwd_kernel, chunk=chunk, n_chunk=n_chunk...]
    dot_general x54 -> x18, matrix products: 666 us -> 44.1 us  [the longest x14 38.2 us: mm(): return lax.dot_general(lhs, rhs, dims, preferred_element_type=F32)]
    convert_element_type x15 -> x7, other arithmetic: 264 us -> 6.94 us  [the longest x1 3.82 us: device_step(): jnp.stack([wk_t, wv_t]).astype(F32)[None]]
    all_gather x1 -> x5, waiting for transfers between devices: 21.1 us -> 190 us  [the longest x1 78.5 us: device_step(): lax.all_gather(jnp.stack([wk_t, wv_t]).astype(F32)[None], 'tp', axis=0, t...]
    convert_element_type x6 -> x1, local copies, waits for them, and re-layouts: 117 us -> 0.08 us  [device_step(): pos_all = rows_all[:, n_own, :n_q].reshape(-1).astype(jnp.int32)]
    add_any x4 -> x1, other arithmetic: 107 us -> 0.17 us  [rotate(): second_half * sin_a]
    reduce_sum x6 -> x2, other arithmetic: 98.8 us -> 2.14 us  [norm_rows(): values * lax.rsqrt(jnp.mean(values * values, axis=-1, keepdims=True) + NO...]
  transfers between devices with their start and end apart: 8 -> 10, of which waited for: 8 -> 8; matrix products, arithmetic and copies ran while one was open for 16% -> 8% of each run, Pallas kernels for 0% -> 1%
where the time goes in v1:
time: 1090 us
  Pallas kernels  637 us (58%)
  waiting for transfers between devices  259 us (24%)
  local copies, waits for them, and re-layouts  62.1 us (6%)
  matrix products  46.1 us (4%)
  other arithmetic  45.3 us (4%)
  blocking collectives  18.1 us (2%)
  between operations  15.8 us (1%)
    pallas_call x2, Pallas kernels, run_backward(): pl.pallas_call(functools.partial(bwd_kernel, chunk=chunk, n_chunk=n_chunk...  451 us
    pallas_call x2, Pallas kernels, run_forward(): pl.pallas_call(functools.partial(fwd_kernel, chunk=chunk, n_chunk=n_chunk...  152 us
    all_gather x1, waiting for transfers between devices, device_step(): lax.all_gather(jnp.stack([wk_t, wv_t]).astype(F32)[None], 'tp', axis=0, t...  78.5 us
    psum x1, waiting for transfers between devices, device_step(): lax.psum(jnp.concatenate([d_wk_t, jnp.pad(gains, ((0, 5), (0, 0)))]), 'dp')  58.6 us
    all_gather x1, waiting for transfers between devices, device_step(): lax.all_gather(jnp.concatenate([x_last, attn_out], axis=1), 'dp', axis=0,...  39.2 us
    dot_general x14, matrix products, mm(): return lax.dot_general(lhs, rhs, dims, preferred_element_type=F32)  38.2 us
    all_gather x1, waiting for transfers between devices, device_step(): lax.all_gather(jnp.concatenate([jnp.concatenate([h_mid, h_out], axis=1),...  29.5 us
  transfers between devices with their start and end apart: 10, of which 8 were waited for; matrix products, arithmetic and copies ran while one was open for 8% of the time, Pallas kernels for 1%

profile of v1, /device:TPU:0, one launch (start us, length us, event | category | flops | bytes accessed | tf_op | source)
XLA Modules:
  0.0 1091.8 jit_solution(1398607950942312488)
XLA Ops:
  33.2 131.8 %attend_forward.3 = f32[64,8,1024]{2,1,0:T(8,128)} custom-call(s32[64]{0:T(128)} %len_ref.11, bf16[64,512,1024]{2,1,0:T(8,128)(2,1)} %h_ref.7, bf16[512,1024]{1,0:T(8,128)(2,1)} %bitcast.119, f32[64,8,128]{2,1,0:T(8,128)} %slice.162.q_ref, f32[1,1024]{1,0:T(1,128)} %bitcast.141, f32[128,128]{1,0:T(8,128)} %broadcast_in_dim.51.gk_ref, ...), custom_call_target="tpu_custom_call" | custom-call | flops 34359738368 | bytes 67108864 | tf_op jit(solution)/shard_map/attend_forward/pallas_call | solution.py:295
  167.4 20.6 %attend_forward.2 = f32[16,8,1024]{2,1,0:T(8,128)} custom-call(s32[16]{0:T(128)} %len_ref.10, bf16[16,512,1024]{2,1,0:T(8,128)(2,1)} %h_ref.6, bf16[512,1024]{1,0:T(8,128)(2,1)} %bitcast.120, f32[16,8,128]{2,1,0:T(8,128)} %slice.161.q_ref, f32[1,1024]{1,0:T(1,128)} %bitcast.142, f32[128,128]{1,0:T(8,128)} %broadcast_in_dim.51.gk_ref, ...), custom_call_target="tpu_custom_call" | custom-call | flops 2147483648 | bytes 4194304 | tf_op jit(solution)/shard_map/attend_forward/pallas_call | solution.py:295
  197.7 5.0 collective-permute-done
  205.3 4.0 fusion.24
  211.3 5.0 collective-permute-done.1
  224.6 8.3 all_gather.27
  234.9 29.5 %all-gather.15.cloned.1.call-done = f32[704,2048]{1,0:T(8,128)} async-done(((f32[88,2048]{1,0:T(8,128)}), f32[704,2048]{1,0:T(8,128)}) %all-gather.15.cloned.1.call-update) | async-done | bytes 5767184 | tf_op jit(solution)/shard_map/all_gather | solution.py:450
  298.3 78.5 %all-gather.7.cloned.1.call-done = f32[2,2,512,1024]{3,2,1,0:T(8,128)} async-done(((f32[1,2,512,1024]{3,2,1,0:T(8,128)}), f32[2,2,512,1024]{3,2,1,0:T(8,128)}) %all-gather.7.cloned.1.call-update) | async-done | bytes 8388624 | tf_op jit(solution)/shard_map/all_gather | solution.py:411
  376.8 8.5 fusion.91
  389.6 9.9 all_gather.28.d_ref
  399.4 12.9 %value_rows.1 = f32[80,16384]{1,0:T(8,128)} custom-call(f32[80,2048]{1,0:T(8,128)} %all_gather.28.d_ref, f32[8,128,1024]{2,1,0:T(8,128)} %bitcast.115), custom_call_target="tpu_custom_call" | custom-call | flops 335544320 | bytes 5242880 | tf_op jit(solution)/shard_map/value_rows/pallas_call | solution.py:260
  414.6 4.4 copy.105
  420.5 398.7 %attend_backward.3 = (bf16[64,512,1024]{2,1,0:T(8,128)(2,1)}, f32[512,1024]{1,0:T(8,128)}, f32[128,128]{1,0:T(8,128)}, f32[8,1024]{1,0:T(8,128)}, f32[64,16,1024]{2,1,0:T(8,128)}, /*index=5*/f32[64,1,1024]{2,1,0:T(1,128)}) custom-call(s32[64]{0:T(128)} %len_ref.11, s32[1]{0:T(128)} %bitcast.16.tp_ref, bf16[64,512,1024]{2,1,0:T(8,128)(2,1)} %h_ref.7, ...), custom_call_target="tpu_custom_call" | custom-call | flops 171798691840 | bytes 134217728 | tf_op jit(solution)/shard_map/attend_backward/pallas_call | solution.py:321
  819.2 52.5 %attend_backward.2 = (bf16[16,512,1024]{2,1,0:T(8,128)(2,1)}, f32[512,1024]{1,0:T(8,128)}, f32[128,128]{1,0:T(8,128)}, f32[8,1024]{1,0:T(8,128)}, f32[16,16,1024]{2,1,0:T(8,128)}, /*index=5*/f32[16,1,1024]{2,1,0:T(1,128)}) custom-call(s32[16]{0:T(128)} %len_ref.10, s32[1]{0:T(128)} %bitcast.16.tp_ref, bf16[16,512,1024]{2,1,0:T(8,128)(2,1)} %h_ref.6, ...), custom_call_target="tpu_custom_call" | custom-call | flops 10737418240 | bytes 8388608 | tf_op jit(solution)/shard_map/attend_backward/pallas_call | solution.py:321
  895.8 6.5 fusion.95
  902.3 4.6 fusion.96
  906.9 4.8 fusion.17
  916.6 5.1 patch_last_rows.3
  921.7 58.6 %all-reduce.9.cloned.1.call-done = (f32[520,1024]{1,0:T(8,128)}, f32[1024,512]{1,0:T(8,128)}) async-done(((f32[520,1024]{1,0:T(8,128)}, f32[1024,512]{1,0:T(8,128)}), (f32[520,1024]{1,0:T(8,128)}, f32[1024,512]{1,0:T(8,128)})) %all-reduce.9.cloned.1.call-update) | async-done | bytes 4227088 | tf_op jit(solution)/shard_map/psum | solution.py:519
  986.6 21.4 %all-gather.11.cloned.1.call-done.b_ref = f32[640,1024]{1,0:T(8,128)} async-done(((f32[80,1024]{1,0:T(8,128)}), f32[640,1024]{1,0:T(8,128)}) %all-gather.11.cloned.1.call-update) | async-done | bytes 2621456 | tf_op jit(solution)/shard_map/all_gather | solution.py:516
  1008.0 39.2 %all-gather.9.cloned.1.call-done.a_ref = f32[640,2048]{1,0:T(8,128)} async-done(((f32[80,2048]{1,0:T(8,128)}), f32[640,2048]{1,0:T(8,128)}) %all-gather.9.cloned.1.call-update) | async-done | bytes 5242896 | tf_op jit(solution)/shard_map/all_gather | solution.py:451
  1047.2 6.4 outer_sum.2
  1053.6 21.3 %all-gather.13.cloned.1.call-done.b_ref = f32[640,1024]{1,0:T(8,128)} async-done(((f32[80,1024]{1,0:T(8,128)}), f32[640,1024]{1,0:T(8,128)}) %all-gather.13.cloned.1.call-update) | async-done | bytes 2621456 | tf_op jit(solution)/shard_map/all_gather | solution.py:491
  1074.9 6.5 outer_sum.3
  (295 shorter events, 132.0 us)
Async XLA Ops:
  7.2 198.1 %copy-start = (bf16[1536,1024]{1,0:T(8,128)(2,1)S(1)}, bf16[1536,1024]{1,0:T(8,128)(2,1)}, u32[]{:S(2)}) copy-start(bf16[1536,1024]{1,0:T(8,128)(2,1)} %param.32) | copy-start | bytes 9437188
  7.2 257.2 %all-gather.15.cloned.1.call-start = ((), (), s32[]{:S(2)}) async-start(), calls=%async_computation.4 | async-start | bytes 6488064 | tf_op jit(solution)/shard_map/all_gather | solution.py:450
  17.9 184.8 %copy-start.26 = (bf16[16,1024]{1,0:T(8,128)(2,1)}, bf16[16,1024]{1,0:T(8,128)(2,1)S(1)}, u32[]{:S(2)}) copy-start(bf16[16,1024]{1,0:T(8,128)(2,1)S(1)} %broadcast_select_fusion.1) | copy-start | bytes 98308
  20.8 6.9 copy-start.7
  21.0 6.6 copy-start.45
  21.1 6.5 copy-start.31
  23.2 6.7 copy-start.53
  167.4 21.9 %copy-start.16 = (bf16[64,8,1024]{2,0,1:T(8,128)(2,1)}, bf16[64,8,1024]{2,0,1:T(8,128)(2,1)S(1)}, u32[]{:S(2)}) copy-start(bf16[64,8,1024]{2,0,1:T(8,128)(2,1)S(1)} %copy.99) | copy-start | bytes 3145732
  167.4 21.9 %copy-start.30 = (bf16[1024,4,128]{2,1,0:T(4,128)(2,1)S(1)}, bf16[1024,4,128]{2,1,0:T(4,128)(2,1)}, u32[]{:S(2)}) copy-start(bf16[1024,4,128]{2,1,0:T(4,128)(2,1)} %reshape.506) | copy-start | bytes 3145732
  189.9 7.8 copy-start.58
  192.1 11.8 %copy-start.4 = (bf16[1024,1536]{1,0:T(8,128)(2,1)S(1)}, bf16[1024,1536]{1,0:T(8,128)(2,1)}, u32[]{:S(2)}) copy-start(bf16[1024,1536]{1,0:T(8,128)(2,1)} %param.30) | copy-start | bytes 9437188
  194.3 8.4 collective-permute-start
  209.3 7.1 collective-permute-start.1
  218.4 158.4 %all-gather.7.cloned.1.call-start = ((), (), s32[]{:S(2)}) async-start(), calls=%async_computation | async-start | bytes 12582912 | tf_op jit(solution)/shard_map/all_gather | solution.py:411
  224.5 9.8 copy-start.59
  224.5 755.7 %all-reduce.9.cloned.1.call-start = ((), (), s32[]{:S(2)}) async-start(), calls=%async_computation.5 | async-start | bytes 8454144 | tf_op jit(solution)/shard_map/psum | solution.py:519
  296.8 90.5 %collective-permute-start.2 = (f32[80,1024]{1,0:T(8,128)S(1)}, f32[80,1024]{1,0:T(8,128)S(1)}, u32[]{:S(2)}, u32[]{:S(2)}) collective-permute-start(f32[80,1024]{1,0:T(8,128)S(1)} %convolution_add_fusion), channel_id=1, source_target_pairs={{0,8},{8,0},{1,9},{9,1},{2,10},{10,2},{3,11},{11,3},{4,12},{12,4},... | collective-permute-start | bytes 983048 | tf_op jit(solution)/shard_map/ppermute | solution.py:395
  388.1 24.2 %copy-start.11 = (f32[80,1024]{1,0:T(8,128)}, f32[80,1024]{1,0:T(8,128)S(1)}, u32[]{:S(2)}) copy-start(f32[80,1024]{1,0:T(8,128)S(1)} %maximum_add_fusion) | copy-start | bytes 983044
  819.2 52.5 %copy-start.15 = (f32[64,16,1024]{2,1,0:T(8,128)S(1)}, f32[64,16,1024]{2,1,0:T(8,128)}, u32[]{:S(2)}) copy-start(f32[64,16,1024]{2,1,0:T(8,128)} %get-tuple-element.54) | copy-start | bytes 12582916
  879.9 9.0 collective-permute-start.3
  891.9 116.1 %all-gather.11.cloned.1.call-start = ((), (), s32[]{:S(2)}) async-start(), calls=%async_computation.2 | async-start | bytes 2949120 | tf_op jit(solution)/shard_map/all_gather | solution.py:516
  893.7 153.5 %all-gather.9.cloned.1.call-start = ((), (), s32[]{:S(2)}) async-start(), calls=%async_computation.1 | async-start | bytes 5898240 | tf_op jit(solution)/shard_map/all_gather | solution.py:451
  894.6 180.3 %all-gather.13.cloned.1.call-start = ((), (), s32[]{:S(2)}) async-start(), calls=%async_computation.3 | async-start | bytes 2949120 | tf_op jit(solution)/shard_map/all_gather | solution.py:491
  1074.9 9.6 copy-start.1
  (56 other events, 174.4 us)
Sparse Core Ops, SparseCore 0:
  218.5 45.9 all-gather.14
  266.5 110.1 all-gather.6
  892.0 88.2 all-reduce.8
  982.0 25.9 all-gather.10
  1010.2 36.9 all-gather.8
  1048.9 25.9 all-gather.12
